TPU v7x, 8 devices: a whole 2x2x1 slice. The times are simulated.
8 devices in a mesh: batch: 2 (over z, y), col: 4 (over x, core).
Axes of the slice: x: 2, y: 2, z: 1, core: 2. Of those that a mesh axis runs over, the one named last changes fastest.
Arguments:
- lower: bfloat16 [10240, 5120], P('batch', 'col'), parts along dimension 0
- rhs: bfloat16 [10240, 32768], P('batch', 'col'), parts along dimension 0
Outputs:
- output: bfloat16 [10240, 32768], P('batch', 'col'), parts along dimension 0
There are 2 independent parts. A program takes and returns all parts, laid end to end along the dimension named above; each array names one.
All inputs are finite; a program needn't handle non-finite values.
Results may differ from a plain program's by a relative error of at most 0.001.
Values are sent between devices in bfloat16 or wider.
A program may use at most 1 GiB of HBM per device.

v0:
```python
import jax
import jax.numpy as jnp
from jax import lax
from jax.sharding import PartitionSpec as P

BLOCK_SIZE = 256


def solution(mesh):
    group_size = mesh.shape["col"]

    def local_product(l_cols, b_cols):
        mat_order, local_width = l_cols.shape
        per_dev = local_width // BLOCK_SIZE
        super_width = group_size * BLOCK_SIZE
        pieces = [l_cols[panel_idx * super_width:, panel_idx * BLOCK_SIZE:(panel_idx + 1) * BLOCK_SIZE] for panel_idx in range(per_dev)]
        packed = jnp.concatenate(pieces, axis=0)
        gathered = lax.all_gather(packed, "col")
        col_bands = []
        offset = 0
        for panel_idx in range(per_dev):
            band_rows = mat_order - panel_idx * super_width
            panel_band = gathered[:, offset:offset + band_rows, :]
            offset = offset + band_rows
            panel_band = jnp.transpose(panel_band, (1, 0, 2)).reshape(band_rows, super_width)
            col_bands.append(jnp.pad(panel_band, ((panel_idx * super_width, 0), (0, 0))))
        natural = jnp.concatenate(col_bands, axis=1)
        out_rows = []
        for row_idx in range(mat_order // BLOCK_SIZE):
            row_end = (row_idx + 1) * BLOCK_SIZE
            strip = natural[row_idx * BLOCK_SIZE:row_end, :row_end]
            block_out = jnp.dot(strip, b_cols[:row_end], preferred_element_type=jnp.float32)
            out_rows.append(block_out.astype(jnp.bfloat16))
        return jnp.concatenate(out_rows, axis=0)

    return jax.shard_map(local_product, mesh=mesh, in_specs=(P("batch", "col"), P("batch", "col")), out_specs=P("batch", "col"), check_vma=False)
```

profile of v0, /device:TPU:0, one launch (start us, length us, event | category | flops | bytes accessed | tf_op | source)
XLA Modules:
  0.0 740.3 jit_solution(3161389292372325365)
XLA Ops:
  19.8 190.6 %all-gather.3.cloned.1.call-done = bf16[61440,256]{1,0:T(8,128)(2,1)} async-done(((bf16[15360,256]{1,0:T(8,128)(2,1)}), bf16[61440,256]{1,0:T(8,128)(2,1)}) %all-gather.3.cloned.1.call-update) | async-done | bytes 31457296 | tf_op jit(solution)/shard_map/all_gather | solution.py:18
  216.5 5.8 slice_bitcast_fusion.2
  222.3 7.2 slice_bitcast_fusion.1
  229.5 8.7 %slice_bitcast_fusion = bf16[5120,4,256]{2,0,1:T(8,128)(2,1)} fusion(bf16[4,15360,256]{2,1,0:T(8,128)(2,1)} %bitcast.42), kind=kLoop, calls=%fused_computation.34 | loop fusion | bytes 20971520 | tf_op jit(solution)/shard_map/transpose | solution.py:25
  238.2 14.3 %copy.3 = bf16[5120,4,256]{0,2,1:T(8,128)(2,1)} copy(bf16[5120,4,256]{2,0,1:T(8,128)(2,1)} %slice_bitcast_fusion) | data formatting | bytes 20971520 | tf_op jit(solution)/shard_map/transpose | solution.py:25
  255.0 6.3 copy.7
  261.2 8.6 %copy.6 = bf16[3072,4,256]{0,2,1:T(8,128)(2,1)} copy(bf16[3072,4,256]{2,0,1:T(8,128)(2,1)} %slice_bitcast_fusion.2) | data formatting | bytes 12582912 | tf_op jit(solution)/shard_map/transpose | solution.py:25
  269.9 11.3 %copy.5 = bf16[4096,4,256]{0,2,1:T(8,128)(2,1)} copy(bf16[4096,4,256]{2,0,1:T(8,128)(2,1)} %slice_bitcast_fusion.1) | data formatting | bytes 16777216 | tf_op jit(solution)/shard_map/transpose | solution.py:25
  281.4 8.7 %constant_dynamic-update-slice_fusion.1 = bf16[5120,5120]{0,1:T(8,128)(2,1)} fusion(bf16[5120,1024]{0,1:T(8,128)(2,1)} %bitcast.19), kind=kLoop, calls=%fused_computation.151 | loop fusion | bytes 20971520
  290.1 5.6 fusion.87
  295.6 8.0 %fusion.83 = bf16[5120,8192]{1,0:T(8,128)(2,1)} fusion(bf16[5120,8192]{1,0:T(8,128)(2,1)} %fusion.87, bf16[5120,8192]{1,0:T(8,128)(2,1)} %param.3, bf16[5120,1024]{0,1:T(8,128)(2,1)} %bitcast.21), kind=kOutput, calls=%fused_computation.55 | convolution fusion | flops 2149580800 | bytes 12845056 | tf_op jit(solution)/shard_map/dot_general | solution.py:32
  303.6 10.3 %fusion.136 = bf16[5120,8192]{1,0:T(8,128)(2,1)} fusion(bf16[5120,8192]{1,0:T(8,128)(2,1)} %fusion.83, bf16[5120,8192]{1,0:T(8,128)(2,1)} %param.3, bf16[5120,1024]{0,1:T(8,128)(2,1)} %bitcast.22), kind=kOutput, calls=%fused_computation.75 | convolution fusion | flops 3223322624 | bytes 17170432 | tf_op jit(solution)/shard_map/dot_general | solution.py:32
  314.0 9.0 %constant_dynamic-update-slice_fusion = (bf16[5120,5120]{0,1:T(8,128)(2,1)}, bf16[5120,1024]{0,1:T(8,128)(2,1)}) fusion(bf16[5120,5120]{0,1:T(8,128)(2,1)} %constant_dynamic-update-slice_fusion.1, bf16[4096,1024]{0,1:T(8,128)(2,1)S(1)} %bitcast.37), kind=kLoop, calls=%fused_computation.150 | loop fusion | bytes 29360128
  323.0 12.4 %fusion.133 = bf16[5120,8192]{1,0:T(8,128)(2,1)} fusion(bf16[5120,8192]{1,0:T(8,128)(2,1)} %fusion.136, bf16[256,1024]{0,1:T(8,128)(2,1)S(1)} %bitcast.46, bf16[5120,8192]{1,0:T(8,128)(2,1)} %param.3), kind=kOutput, calls=%fused_computation.74 | convolution fusion | flops 4297064448 | bytes 21495808 | tf_op jit(solution)/shard_map/dot_general | solution.py:32
  335.4 11.4 %fusion.130 = bf16[5120,8192]{1,0:T(8,128)(2,1)} fusion(bf16[5120,8192]{1,0:T(8,128)(2,1)} %fusion.133, bf16[5120,8192]{1,0:T(8,128)(2,1)} %param.3, bf16[5120,1024]{0,1:T(8,128)(2,1)} %get-tuple-element.6, bf16[5120,1024]{0,1:T(8,128)(2,1)} %bitcast.23), kind=kOutput, calls=%fused_computation.73 | convolution fusion | flops 5372116992 | bytes 46137344 | tf_op jit(solution)/shard_map/dot_general | solution.py:32
  346.8 13.2 %fusion.127 = bf16[5120,8192]{1,0:T(8,128)(2,1)} fusion(bf16[5120,8192]{1,0:T(8,128)(2,1)} %fusion.130, bf16[5120,8192]{1,0:T(8,128)(2,1)} %param.3, bf16[5120,1024]{0,1:T(8,128)(2,1)} %get-tuple-element.6, bf16[5120,1024]{0,1:T(8,128)(2,1)} %bitcast.24), kind=kOutput, calls=%fused_computation.72 | convolution fusion | flops 6446120960 | bytes 50331648 | tf_op jit(solution)/shard_map/dot_general | solution.py:32
  360.1 15.2 %fusion.124 = bf16[5120,8192]{1,0:T(8,128)(2,1)} fusion(bf16[5120,8192]{1,0:T(8,128)(2,1)} %fusion.127, bf16[5120,8192]{1,0:T(8,128)(2,1)} %param.3, bf16[5120,1024]{0,1:T(8,128)(2,1)} %get-tuple-element.6, bf16[5120,1024]{0,1:T(8,128)(2,1)} %bitcast.25), kind=kOutput, calls=%fused_computation.71 | convolution fusion | flops 7520124928 | bytes 54525952 | tf_op jit(solution)/shard_map/dot_general | solution.py:32
  375.3 16.8 %fusion.121 = bf16[5120,8192]{1,0:T(8,128)(2,1)} fusion(bf16[5120,8192]{1,0:T(8,128)(2,1)} %fusion.124, bf16[5120,8192]{1,0:T(8,128)(2,1)} %param.3, bf16[5120,1024]{0,1:T(8,128)(2,1)} %get-tuple-element.6, bf16[5120,1024]{0,1:T(8,128)(2,1)} %bitcast.26), kind=kOutput, calls=%fused_computation.70 | convolution fusion | flops 8594128896 | bytes 58720256 | tf_op jit(solution)/shard_map/dot_general | solution.py:32
  392.1 11.4 %pad_dynamic-update-slice_fusion.2 = (bf16[5120,5120]{0,1:T(8,128)(2,1)}, bf16[5120,1024]{0,1:T(8,128)(2,1)}) fusion(bf16[5120,5120]{0,1:T(8,128)(2,1)} %get-tuple-element.5, bf16[3072,1024]{0,1:T(8,128)(2,1)} %bitcast.43), kind=kLoop, calls=%fused_computation.139 | loop fusion | bytes 27262976
  403.4 18.3 %fusion.118 = bf16[5120,8192]{1,0:T(8,128)(2,1)} fusion(bf16[5120,8192]{1,0:T(8,128)(2,1)} %fusion.121, bf16[5120,8192]{1,0:T(8,128)(2,1)} %param.3, bf16[5120,1024]{0,1:T(8,128)(2,1)} %get-tuple-element.8, bf16[5120,1024]{0,1:T(8,128)(2,1)} %get-tuple-element.6, bf16[5120,1024]{0,1:T(8,128)(2,1)} %bitcast.27), kind=kOutput, calls=%fused_computation.69 | convolution fusion | flops 9669312512 | bytes 73400320 | tf_op jit(solution)/shard_map/dot_general | solution.py:32
  421.7 20.1 %fusion.115 = bf16[5120,8192]{1,0:T(8,128)(2,1)} fusion(bf16[5120,8192]{1,0:T(8,128)(2,1)} %fusion.118, bf16[5120,8192]{1,0:T(8,128)(2,1)} %param.3, bf16[5120,1024]{0,1:T(8,128)(2,1)} %get-tuple-element.8, bf16[5120,1024]{0,1:T(8,128)(2,1)} %get-tuple-element.6, bf16[5120,1024]{0,1:T(8,128)(2,1)} %bitcast.28), kind=kOutput, calls=%fused_computation.68 | convolution fusion | flops 10743447552 | bytes 77594624 | tf_op jit(solution)/shard_map/dot_general | solution.py:32
  441.8 21.3 %fusion.112 = bf16[5120,8192]{1,0:T(8,128)(2,1)} fusion(bf16[5120,8192]{1,0:T(8,128)(2,1)} %fusion.115, bf16[5120,8192]{1,0:T(8,128)(2,1)} %param.3, bf16[5120,1024]{0,1:T(8,128)(2,1)} %get-tuple-element.8, bf16[5120,1024]{0,1:T(8,128)(2,1)} %get-tuple-element.6, bf16[5120,1024]{0,1:T(8,128)(2,1)} %bitcast.29), kind=kOutput, calls=%fused_computation.67 | convolution fusion | flops 11817582592 | bytes 81788928 | tf_op jit(solution)/shard_map/dot_general | solution.py:32
  463.1 23.0 %fusion.109 = bf16[5120,8192]{1,0:T(8,128)(2,1)} fusion(bf16[5120,8192]{1,0:T(8,128)(2,1)} %fusion.112, bf16[5120,8192]{1,0:T(8,128)(2,1)} %param.3, bf16[5120,1024]{0,1:T(8,128)(2,1)} %get-tuple-element.8, bf16[5120,1024]{0,1:T(8,128)(2,1)} %get-tuple-element.6, bf16[5120,1024]{0,1:T(8,128)(2,1)} %bitcast.30), kind=kOutput, calls=%fused_computation.66 | convolution fusion | flops 12891717632 | bytes 85983232 | tf_op jit(solution)/shard_map/dot_general | solution.py:32
  486.1 10.5 %pad_dynamic-update-slice_fusion.1 = (bf16[5120,5120]{0,1:T(8,128)(2,1)}, bf16[5120,1024]{0,1:T(8,128)(2,1)}) fusion(bf16[5120,5120]{0,1:T(8,128)(2,1)} %get-tuple-element.7, bf16[2048,1024]{0,1:T(8,128)(2,1)} %bitcast.44), kind=kLoop, calls=%fused_computation.99 | loop fusion | bytes 25165824
  496.5 23.4 %fusion.106 = bf16[5120,8192]{1,0:T(8,128)(2,1)} fusion(bf16[5120,8192]{1,0:T(8,128)(2,1)} %fusion.109, bf16[5120,8192]{1,0:T(8,128)(2,1)} %param.3, bf16[5120,1024]{0,1:T(8,128)(2,1)} %get-tuple-element.10, bf16[5120,1024]{0,1:T(8,128)(2,1)} %get-tuple-element.8, bf16[5120,1024]{0,1:T(8,128)(2,1)} %get-tuple-element.6, bf16[5120,1024]{0,1:T(8,128)(2,1)} %bitcast.31), kind=kOutput, calls=%fused_computation.65 | convolution fusion | flops 13967556608 | bytes 100663296 | tf_op jit(solution)/shard_map/dot_general | solution.py:32
  520.0 24.9 %fusion.103 = bf16[5120,8192]{1,0:T(8,128)(2,1)} fusion(bf16[5120,8192]{1,0:T(8,128)(2,1)} %fusion.106, bf16[5120,8192]{1,0:T(8,128)(2,1)} %param.3, bf16[5120,1024]{0,1:T(8,128)(2,1)} %get-tuple-element.10, bf16[5120,1024]{0,1:T(8,128)(2,1)} %get-tuple-element.8, bf16[5120,1024]{0,1:T(8,128)(2,1)} %get-tuple-element.6, bf16[5120,1024]{0,1:T(8,128)(2,1)} %bitcast.32), kind=kOutput, calls=%fused_computation.64 | convolution fusion | flops 15041822720 | bytes 104857600 | tf_op jit(solution)/shard_map/dot_general | solution.py:32
  544.9 26.4 %fusion.100 = bf16[5120,8192]{1,0:T(8,128)(2,1)} fusion(bf16[5120,8192]{1,0:T(8,128)(2,1)} %fusion.103, bf16[5120,8192]{1,0:T(8,128)(2,1)} %param.3, bf16[5120,1024]{0,1:T(8,128)(2,1)} %get-tuple-element.10, bf16[5120,1024]{0,1:T(8,128)(2,1)} %get-tuple-element.8, bf16[5120,1024]{0,1:T(8,128)(2,1)} %get-tuple-element.6, bf16[5120,1024]{0,1:T(8,128)(2,1)} %bitcast.33), kind=kOutput, calls=%fused_computation.63 | convolution fusion | flops 16116088832 | bytes 109051904 | tf_op jit(solution)/shard_map/dot_general | solution.py:32
  571.3 28.2 %fusion.97 = bf16[5120,8192]{1,0:T(8,128)(2,1)} fusion(bf16[5120,8192]{1,0:T(8,128)(2,1)} %fusion.100, bf16[5120,8192]{1,0:T(8,128)(2,1)} %param.3, bf16[5120,1024]{0,1:T(8,128)(2,1)} %get-tuple-element.10, bf16[5120,1024]{0,1:T(8,128)(2,1)} %get-tuple-element.8, bf16[5120,1024]{0,1:T(8,128)(2,1)} %get-tuple-element.6, bf16[5120,1024]{0,1:T(8,128)(2,1)} %bitcast.34), kind=kOutput, calls=%fused_computation.62 | convolution fusion | flops 17190354944 | bytes 113246208 | tf_op jit(solution)/shard_map/dot_general | solution.py:32
  604.8 29.4 %fusion.94 = bf16[5120,8192]{1,0:T(8,128)(2,1)} fusion(bf16[5120,8192]{1,0:T(8,128)(2,1)} %fusion.97, bf16[5120,8192]{1,0:T(8,128)(2,1)} %param.3, bf16[5120,5120]{0,1:T(8,128)(2,1)} %pad_dynamic-update-slice_fusion), kind=kOutput, calls=%fused_computation.61 | convolution fusion | flops 18255708160 | bytes 77725696 | tf_op jit(solution)/shard_map/dot_general | solution.py:32
  634.2 31.7 %fusion.91 = bf16[5120,8192]{1,0:T(8,128)(2,1)} fusion(bf16[5120,8192]{1,0:T(8,128)(2,1)} %fusion.94, bf16[5120,8192]{1,0:T(8,128)(2,1)} %param.3, bf16[5120,5120]{0,1:T(8,128)(2,1)} %pad_dynamic-update-slice_fusion), kind=kOutput, calls=%fused_computation.60 | convolution fusion | flops 19329449984 | bytes 82051072 | tf_op jit(solution)/shard_map/dot_general | solution.py:32
  665.9 33.5 %fusion.88 = bf16[5120,8192]{1,0:T(8,128)(2,1)} fusion(bf16[5120,8192]{1,0:T(8,128)(2,1)} %fusion.91, bf16[5120,8192]{1,0:T(8,128)(2,1)} %param.3, bf16[5120,5120]{0,1:T(8,128)(2,1)} %pad_dynamic-update-slice_fusion), kind=kOutput, calls=%fused_computation.59 | convolution fusion | flops 20403191808 | bytes 86376448 | tf_op jit(solution)/shard_map/dot_general | solution.py:32
  699.3 33.8 %fusion.82 = bf16[5120,8192]{1,0:T(8,128)(2,1)} fusion(bf16[5120,8192]{1,0:T(8,128)(2,1)} %fusion.88, bf16[5120,8192]{1,0:T(8,128)(2,1)} %param.3, bf16[5120,5120]{0,1:T(8,128)(2,1)} %pad_dynamic-update-slice_fusion), kind=kOutput, calls=%fused_computation.53 | convolution fusion | flops 21476933632 | bytes 90701824 | tf_op jit(solution)/shard_map/dot_general | solution.py:32
  (21 shorter events, 27.2 us)
Async XLA Ops:
  6.5 203.9 %all-gather.3.cloned.1.call-start = ((), (), s32[]{:S(2)}) async-start(), calls=%async_computation | async-start | bytes 39321600 | tf_op jit(solution)/shard_map/all_gather | solution.py:18
  269.9 11.3 %slice-start = ((bf16[5120,4,256]{2,0,1:T(8,128)(2,1)}), bf16[256,4,256]{2,0,1:T(8,128)(2,1)S(1)}, s32[]{:S(2)}) async-start(bf16[5120,4,256]{2,0,1:T(8,128)(2,1)} %slice_bitcast_fusion), calls=%async_computation.1 | async-start | bytes 1048576 | tf_op jit(solution)/shard_map/slice | solution.py:31
  295.6 18.4 %slice-start.1 = ((s8[8388608]{0:T(1024)(128)(4,1)}), s8[4194304]{0:T(1024)(128)(4,1)S(1)}, s32[]{:S(2)}) async-start(s8[8388608]{0:T(1024)(128)(4,1)} %bitcast.35), calls=%async_computation.2 | async-start | bytes 8388608
  303.6 10.4 %slice-start.2 = ((s8[8388608]{0:T(1024)(128)(4,1)}), s8[4194304]{0:T(1024)(128)(4,1)S(1)}, s32[]{:S(2)}) async-start(s8[8388608]{0:T(1024)(128)(4,1)} %bitcast.35), calls=%async_computation.3 | async-start | bytes 8388608
  571.3 28.2 %copy-start = (bf16[1024,4,256]{0,2,1:T(8,128)(2,1)S(1)}, bf16[1024,4,256]{0,2,1:T(8,128)(2,1)}, u32[]{:S(2)}) copy-start(bf16[1024,4,256]{0,2,1:T(8,128)(2,1)} %copy.8) | copy-start | bytes 6291460
Sparse Core Ops, SparseCore 0:
  19.9 190.4 all-gather.2
where the time goes:
time: 745 us; the launch traced here: 740 us
  matrix products  407 us (55%)
  waiting for transfers between devices  191 us (26%)
  local copies, waits for them, and re-layouts  129 us (17%)
  between operations  13.7 us (2%)
    dot_general x20, matrix products, local_product(): jnp.dot(strip, b_cols[:row_end], preferred_element_type=jnp.float32)  407 us
    all_gather x1, waiting for transfers between devices, local_product(): gathered = lax.all_gather(packed, 'col')  191 us
    transpose x10, local copies, waits for them, and re-layouts, local_product(): jnp.transpose(panel_band, (1, 0, 2)).reshape(band_rows, super_width)  70.7 us
    unnamed x14, local copies, waits for them, and re-layouts  50.9 us
  transfers between devices with their start and end apart: 1, of which 1 were waited for; matrix products, arithmetic and copies ran while one was open for 0% of the time, Pallas kernels for 0%

commit v1 on v0

v1 whole, which is shorter than its diff:
```python
import functools

import jax
import jax.numpy as jnp
from jax import lax
from jax.experimental import pallas as pl
from jax.experimental.pallas import tpu as pltpu
from jax.sharding import PartitionSpec as P

BF = jnp.bfloat16
F32 = jnp.float32
BLK = 256
SUP = 4 * BLK
TN = 512
NSUP = 5
NT = 16
NT2 = 8
ROWS = (0, 1, 2, 3)

CHUNKS = [(s, t) for s in (4, 3, 2, 1, 0) for t in range(s + 1)]
CHUNK_ID = {st: i for i, st in enumerate(CHUNKS)}
LG_BASE = {0: 0, 1: 4, 2: 12}


def diag_passes(base):
    return [(base + 1, (1, 2, 3)), (base + 2, (2, 3)), (base + 3, (3,))]


def run_tiles(accs, subs, lhs_of, rhs_of, emit, top, n_tiles):
    flat = [(s, k, rows) for s, passes in enumerate(subs) for k, rows in passes]

    def push(k, j):
        for m in range(2):
            pltpu.matmul_push_rhs(rhs_of(k, m, j), staging_register=0, mxu_index=m)

    def acc_pass(s, k, rows):
        for i, r in enumerate(rows):
            lhs = lhs_of(s, k, r)
            for m in range(2):
                pltpu.matmul_acc_lhs(accs[m][r], lhs, load_staged_rhs=0 if i == 0 else None)

    def pops(s, j):
        for r in ROWS:
            for m in range(2):
                emit(s, j, r, m, pltpu.matmul_pop(accs[m][r]))

    def body(j, carry):
        top(j)
        acc_pass(*flat[-1])
        push(flat[0][1], j + 1)
        pops(flat[-1][0], j)
        for i, (s, k, rows) in enumerate(flat[:-1]):
            acc_pass(s, k, rows)
            push(flat[i + 1][1], j + 1)
            if flat[i + 1][0] != s:
                pops(s, j + 1)
        return carry

    lax.fori_loop(-1, n_tiles - 1, body, 0)
    top(n_tiles - 1)
    acc_pass(*flat[-1])
    pops(flat[-1][0], n_tiles - 1)


def when(cond, fn):
    if isinstance(cond, bool):
        if cond:
            fn()
    else:
        pl.when(cond)(fn)


def cols(j):
    return pl.ds(j * TN, TN) if isinstance(j, int) else pl.ds(pl.multiple_of(j * TN, TN), TN)


def gather_kernel(l_ref, b_ref, lg_ref, x1_ref, x2_ref, pf_ref, la, lb, lc, bbuf, pbuf, obuf, own_sem, dsend, drecv, xsend, xrecv,
                  fsend, frecv, bsem, psem, osem, gsem):
    me = lax.axis_index("col")
    core = lax.rem(me, 2)
    chip = me // 2
    sib = me + 1 - 2 * core
    oth = lax.rem(me + 2, 4)
    sib_oth = lax.rem(sib + 2, 4)
    strips = {4: la, 3: lb, 2: lc}

    def own_src(s, t):
        return l_ref.at[pl.ds(SUP * s, SUP), pl.ds(BLK * t, BLK)]

    def place(s, t, dev, far):
        if s not in strips:
            return lg_ref.at[LG_BASE[s] + 4 * t + dev]
        if t == s:
            slot = 4 * s + dev
        else:
            slot = (2 * s if far else 0) + 2 * t + lax.rem(dev, 2)
        return strips[s].at[:, pl.ds(pl.multiple_of(slot * BLK, BLK), BLK)]

    def own_copy(s, t):
        return pltpu.make_async_copy(own_src(s, t), place(s, t, me, False), own_sem.at[CHUNK_ID[s, t]])

    def remote(src, dst, send, recv, dev):
        return pltpu.make_async_remote_copy(src_ref=src, dst_ref=dst, send_sem=send, recv_sem=recv, device_id={"col": dev},
                                            device_id_type=pl.DeviceIdType.MESH)

    def to_sib(s, t):
        i = CHUNK_ID[s, t]
        return remote(own_src(s, t), place(s, t, me, False), dsend.at[i], drecv.at[i], sib)

    def to_oth(s, t):
        i = CHUNK_ID[s, t]
        return remote(own_src(s, t), place(s, t, me, True), xsend.at[i], xrecv.at[i], oth)

    def forward(s, t):
        i = CHUNK_ID[s, t]
        here = place(s, t, oth, True)
        return remote(here, here, fsend.at[i], frecv.at[i], sib)

    def from_sib(s, t):
        i = CHUNK_ID[s, t]
        here = place(s, t, sib, False)
        return remote(here, here, dsend.at[i], drecv.at[i], sib)

    def from_oth(s, t):
        i = CHUNK_ID[s, t]
        here = place(s, t, oth, True)
        return remote(here, here, xsend.at[i], xrecv.at[i], oth)

    def from_fwd(s, t):
        i = CHUNK_ID[s, t]
        here = place(s, t, sib_oth, True)
        return remote(here, here, fsend.at[i], frecv.at[i], sib)

    def pass_on(s, t):
        from_oth(s, t).wait_recv()
        forward(s, t).start()

    jobs = [(4, "part", NT), (3, "part", NT), (4, "rest", NT), (3, "rest", NT), (2, "all", NT2)]
    passes = {"part": lambda s: 2 * s * 512, "rest": lambda s: 2 * s * 512 + 1280, "all": lambda s: 4 * s * 512 + 1280}
    events = [dict() for _ in jobs]
    clock, todo = 6.0, list(enumerate(CHUNKS))
    for q, (s, kind, n) in enumerate(jobs):
        for j in range(n):
            if todo and clock > 5.0 + 11.3 * (todo[0][0] + 1) + 1.5:
                events[q][j] = todo.pop(0)[1]
            clock += passes[kind](s) / 1850.0
    left = [st for _, st in todo]

    def b_copies(q, j, slot):
        s, kind, _ = jobs[q]
        dst = bbuf.at[slot]
        if kind == "part":
            return [pltpu.make_async_copy(b_ref.at[0:s, chip, :, cols(j)], dst.at[0:s], bsem.at[slot, 0])]
        far = pltpu.make_async_copy(b_ref.at[0:s, 1 - chip, :, cols(j)], dst.at[0:s], bsem.at[slot, 0])
        if kind == "rest":
            return [far, pltpu.make_async_copy(b_ref.at[s, :, :, cols(j)], dst.at[pl.ds(s, 2)], bsem.at[slot, 1])]
        return [
            pltpu.make_async_copy(b_ref.at[0:s, chip, :, cols(j)], dst.at[0:s], bsem.at[slot, 0]),
            pltpu.make_async_copy(b_ref.at[0:s, 1 - chip, :, cols(j)], dst.at[pl.ds(s, s)], bsem.at[slot, 2]),
            pltpu.make_async_copy(b_ref.at[s, :, :, cols(j)], dst.at[pl.ds(2 * s, 2)], bsem.at[slot, 1]),
        ]

    def run_job(q):
        s, kind, n = jobs[q]
        lbuf = strips[s]
        nxt = q + 1 if q + 1 < len(jobs) else None

        def start_b(qq, j, slot):
            for c in b_copies(qq, j, slot):
                c.start()

        def out_copy(j):
            slot = j & 1
            if kind == "part":
                return pltpu.make_async_copy(pbuf.at[slot], pf_ref.at[s - 3, :, cols(j)], osem.at[slot])
            if kind == "rest":
                return pltpu.make_async_copy(obuf.at[slot], x1_ref.at[pl.ds(SUP * (s - 3), SUP), cols(j)], osem.at[slot])
            return pltpu.make_async_copy(obuf.at[slot], x2_ref.at[:, cols(j)], osem.at[slot])

        def part_copy(j):
            slot = j & 1
            return pltpu.make_async_copy(pf_ref.at[s - 3, :, cols(j)], pbuf.at[slot], psem.at[slot])

        def body(j, carry):
            slot = j & 1
            pl.when(j < n - 1)(lambda: start_b(q, j + 1, 1 - slot))
            if nxt is not None:
                pl.when(j == n - 1)(lambda: start_b(nxt, 0, 0))
            if events[q]:
                hit = functools.reduce(jnp.logical_or, [j == jj for jj in events[q]])

                @pl.when(hit)
                def _():
                    for jj, st in events[q].items():
                        pl.when(j == jj)(functools.partial(pass_on, *st))

            pl.when(j >= 1)(lambda: out_copy(j - 1).start())
            pl.when(j >= 2)(lambda: out_copy(j - 2).wait())
            if kind == "rest":
                pl.when(j < n - 1)(lambda: part_copy(j + 1).start())
                part_copy(j).wait()
            for c in b_copies(q, j, slot):
                c.wait()
            base = 0 if kind == "part" else (2 * s if kind == "rest" else 0)
            for r in ROWS:
                rows = slice(r * BLK, (r + 1) * BLK)
                n_k = 2 * s if kind == "part" else (4 * s + r + 1 - base)
                rhs = bbuf[slot, 0:(n_k + 1) // 2].reshape(-1, TN)[0:n_k * BLK]
                v = jnp.dot(lbuf[rows, base * BLK:(base + n_k) * BLK], rhs, preferred_element_type=F32)
                if kind == "part":
                    pbuf[slot, rows, :] = v
                elif kind == "rest":
                    obuf[slot, rows, :] = (v + pbuf[slot, rows, :]).astype(BF)
                else:
                    obuf[slot, rows, :] = v.astype(BF)
            return carry

        if kind == "rest":
            part_copy(0).start()
        lax.fori_loop(0, n, body, 0)
        out_copy(n - 1).start()
        out_copy(n - 2).wait()
        out_copy(n - 1).wait()

    def inner():
        for s in (4, 3, 2):
            for t in range(s + 1):
                own_copy(s, t).start()
        for c in b_copies(0, 0, 0):
            c.start()
        barrier = pltpu.get_barrier_semaphore()
        for dev in (sib, oth):
            pl.semaphore_signal(barrier, inc=1, device_id={"col": dev}, device_id_type=pl.DeviceIdType.MESH)
        pl.semaphore_wait(barrier, 2)
        for t in range(5):
            to_sib(4, t).start()
        for s, t in CHUNKS:
            to_oth(s, t).start()
        for s, t in CHUNKS[5:]:
            to_sib(s, t).start()

        for s, t in CHUNKS[:12]:
            own_copy(s, t).wait()
        for t in range(4):
            from_sib(4, t).wait_recv()
        run_job(0)
        for t in range(3):
            from_sib(3, t).wait_recv()
        run_job(1)
        from_sib(4, 4).wait_recv()
        for t in range(5):
            from_fwd(4, t).wait_recv()
        run_job(2)
        from_sib(3, 3).wait_recv()
        for t in range(4):
            from_fwd(3, t).wait_recv()
        run_job(3)
        for t in range(3):
            from_sib(2, t).wait_recv()
            from_fwd(2, t).wait_recv()
        saves = []
        for k in range(12):
            t, u = k % 4 // 2, k % 2
            kb = k if k >= 8 else 4 * t + 2 * (chip if k < 4 else 1 - chip) + u
            saves.append(pltpu.make_async_copy(lc.at[:, pl.ds(k * BLK, BLK)], lg_ref.at[LG_BASE[2] + kb], gsem.at[k]))
        for c in saves:
            c.start()
        run_job(4)
        for s, t in left:
            pass_on(s, t)
        for c in saves:
            c.wait()
        for s in (1, 0):
            for t in range(s + 1):
                from_sib(s, t).wait_recv()
                from_fwd(s, t).wait_recv()
        for s, t in CHUNKS:
            to_sib(s, t).wait_send()
            to_oth(s, t).wait_send()
            forward(s, t).wait_send()

    inner()


def finish_kernel(l_ref, b_ref, lg_ref, x1_ref, x2_ref, x_ref, lbuf, bbuf, obuf, cbuf, dbuf, lsem, bsem, osem, csem, dsem):
    me = lax.axis_index("col")
    jobs = [(0, NT2, (0, 1)), (NT2, NT - NT2, (0, 1, 2))]

    def l_copies(s):
        base = LG_BASE[s]
        if s == 2:
            return [pltpu.make_async_copy(lg_ref.at[pl.ds(base, 12)], lbuf.at[pl.ds(base, 12)], lsem.at[base])]
        out = []
        for t in range(s + 1):
            for d in range(4):
                at = base + 4 * t + lax.rem(me + d, 4)
                src = l_ref.at[pl.ds(SUP * s, SUP), pl.ds(BLK * t, BLK)] if d == 0 else lg_ref.at[at]
                out.append(pltpu.make_async_copy(src, lbuf.at[at], lsem.at[base + 4 * t + d]))
        return out

    def b_copy(q, j, slot):
        n = 4 * len(jobs[q][2])
        return pltpu.make_async_copy(b_ref.at[0:n, :, cols(jobs[q][0] + j)], bbuf.at[slot, 0:n], bsem.at[slot])

    def run_job(q, accs):
        first, n, sups = jobs[q]
        nxt = q + 1 if q + 1 < len(jobs) else None
        lasts = len(sups) - 1

        def out_copy(u, j):
            slot = j & 1
            return pltpu.make_async_copy(obuf.at[slot, u], x_ref.at[pl.ds(SUP * sups[u], SUP), cols(first + j)], osem.at[slot, u])

        if q == 0:
            rows = SUP // n

            def c_in(j):
                return pltpu.make_async_copy(x2_ref.at[pl.ds(pl.multiple_of(j * rows, rows), rows), :], dbuf.at[j & 1], dsem.at[0, j & 1])

            def c_out(j):
                return pltpu.make_async_copy(
                    dbuf.at[j & 1], x_ref.at[pl.ds(pl.multiple_of(2 * SUP + j * rows, rows), rows), pl.ds(0, NT2 * TN)], dsem.at[1, j & 1])
        else:
            rows = 2 * SUP // n

            def c_in(j):
                return pltpu.make_async_copy(x1_ref.at[pl.ds(pl.multiple_of(j * rows, rows), rows), :], cbuf.at[j & 1], csem.at[0, j & 1])

            def c_out(j):
                return pltpu.make_async_copy(
                    cbuf.at[j & 1], x_ref.at[pl.ds(pl.multiple_of(3 * SUP + j * rows, rows), rows), :], csem.at[1, j & 1])

        def top(j):
            last = isinstance(j, int)
            if not last:
                b_copy(q, j + 1, (j + 1) & 1).wait()
                lo = -1 if q == 0 else 0
                pl.when(jnp.logical_and(j >= lo, j < n - 2))(lambda: b_copy(q, j + 2, j & 1).start())
                if nxt is not None:
                    pl.when(j == n - 2)(lambda: b_copy(nxt, 0, 0).start())
            elif nxt is not None:
                b_copy(nxt, 1, 1).start()
            for u in range(len(sups)):
                if u < lasts:
                    when(True if last else j >= 0, lambda: out_copy(u, j).start())
                    when(True if last else j >= 1, lambda: out_copy(u, j - 1).wait())
                else:
                    when(True if last else j >= 1, lambda: out_copy(u, j - 1).start())
                    when(True if last else j >= 2, lambda: out_copy(u, j - 2).wait())
            if not last:
                pl.when(j >= 1)(lambda: c_out(j - 1).wait())
                c_in(j + 1).start()
            when(True if last else j >= 0, lambda: c_in(j).wait())
            when(True if last else j >= 0, lambda: c_out(j).start())

        def lhs_of(u, k, r):
            return lbuf[LG_BASE[sups[u]] + k, r * BLK:(r + 1) * BLK, :]

        def rhs_of(k, m, j):
            return bbuf[j & 1, k, :, m * BLK:(m + 1) * BLK]

        def emit(u, j, r, m, v):
            obuf[j & 1, u, r * BLK:(r + 1) * BLK, m * BLK:(m + 1) * BLK] = v.astype(BF)

        subs = [diag_passes(4 * s) + [(4 * s, ROWS)] + [(k, ROWS) for k in range(4 * s)] for s in sups]
        run_tiles(accs, subs, lhs_of, rhs_of, emit, top, n)
        out_copy(lasts, n - 1).start()
        c_out(n - 2).wait()
        c_out(n - 1).wait()
        for u in range(len(sups)):
            if u == lasts:
                out_copy(u, n - 2).wait()
            out_copy(u, n - 1).wait()

    def inner(*refs):
        accs = (refs[:4], refs[4:])
        b_copy(0, 0, 0).start()
        for s in (0, 1, 2):
            for c in l_copies(s):
                c.start()
        for s in (0, 1):
            for c in l_copies(s):
                c.wait()
        run_job(0, accs)
        for c in l_copies(2):
            c.wait()
        run_job(1, accs)

    pl.run_scoped(inner, *[pltpu.ACC(m)((BLK, BLK), F32) for m in range(2) for _ in ROWS])


def solution(mesh):
    hbm = pl.BlockSpec(memory_space=pltpu.HBM)
    dma = pltpu.SemaphoreType.DMA

    def local_product(l_cols, b_cols):
        order, width = b_cols.shape
        b4 = b_cols.reshape(NSUP, 2, 2 * BLK, width)
        b3 = b_cols.reshape(4 * NSUP, BLK, width)
        lg, x1, x2, _ = pl.pallas_call(
            gather_kernel,
            out_shape=(
                jax.ShapeDtypeStruct((24, SUP, BLK), BF),
                jax.ShapeDtypeStruct((2 * SUP, width), BF),
                jax.ShapeDtypeStruct((SUP, NT2 * TN), BF),
                jax.ShapeDtypeStruct((2, SUP, width), F32),
            ),
            in_specs=[hbm] * 2,
            out_specs=(hbm,) * 4,
            scratch_shapes=[
                pltpu.VMEM((SUP, 20 * BLK), BF),
                pltpu.VMEM((SUP, 16 * BLK), BF),
                pltpu.VMEM((SUP, 12 * BLK), BF),
                pltpu.VMEM((2, 6, 2 * BLK, TN), BF),
                pltpu.VMEM((2, SUP, TN), F32),
                pltpu.VMEM((2, SUP, TN), BF),
            ] + [dma((15,))] * 7 + [dma((2, 3)), dma((2,)), dma((2,)), dma((12,))],
            compiler_params=pltpu.CompilerParams(vmem_limit_bytes=62 * 1024 * 1024, collective_id=0, has_side_effects=True),
        )(l_cols, b4)
        return pl.pallas_call(
            finish_kernel,
            out_shape=jax.ShapeDtypeStruct((order, width), BF),
            in_specs=[hbm] * 5,
            out_specs=hbm,
            scratch_shapes=[
                pltpu.VMEM((24, SUP, BLK), BF),
                pltpu.VMEM((2, 12, BLK, TN), BF),
                pltpu.VMEM((2, 3, SUP, TN), BF),
                pltpu.VMEM((2, 2 * SUP // (NT - NT2), width), BF),
                pltpu.VMEM((2, SUP // NT2, NT2 * TN), BF),
            ] + [dma((24,)), dma((2,)), dma((2, 3)), dma((2, 2)), dma((2, 2))],
            compiler_params=pltpu.CompilerParams(vmem_limit_bytes=62 * 1024 * 1024),
        )(l_cols, b3, lg, x1, x2)

    return jax.shard_map(local_product, mesh=mesh, in_specs=(P("batch", "col"), P("batch", "col")), out_specs=P("batch", "col"), check_vma=False)
```

time: 745 us -> 281 us (0.38)
  matrix products: 407 us -> 0 us
  Pallas kernels: 0 us -> 280 us
  waiting for transfers between devices: 191 us -> 0 us
  local copies, waits for them, and re-layouts: 129 us -> 0 us
  between operations: 13.7 us -> 0.17 us
    dot_general x20 -> x0, matrix products: 407 us -> none  [local_product(): jnp.dot(strip, b_cols[:row_end], preferred_element_type=jnp.float32)]
    pallas_call x0 -> x2, Pallas kernels: none -> 280 us  [the longest x1 205 us: local_product(): pl.pallas_call(gather_kernel, out_shape=(jax.ShapeDtypeStruct((24, SUP, B...]
    all_gather x1 -> x0, waiting for transfers between devices: 191 us -> none  [local_product(): gathered = lax.all_gather(packed, 'col')]
    transpose x10 -> x0, local copies, waits for them, and re-layouts: 70.7 us -> none  [local_product(): jnp.transpose(panel_band, (1, 0, 2)).reshape(band_rows, super_width)]
    unnamed x14 -> x0, local copies, waits for them, and re-layouts: 50.9 us -> none
  transfers between devices with their start and end apart: 1 -> 0, of which waited for: 1 -> 0; matrix products, arithmetic and copies ran while one was open for 0% -> 0% of each run, Pallas kernels for 0% -> 0%
where the time goes in v1:
time: 281 us; the launch traced here: 280 us
  Pallas kernels  280 us (100%)
    pallas_call x1, Pallas kernels, local_product(): pl.pallas_call(gather_kernel, out_shape=(jax.ShapeDtypeStruct((24, SUP, B...  205 us
    pallas_call x1, Pallas kernels, local_product(): pl.pallas_call(finish_kernel, out_shape=jax.ShapeDtypeStruct((order, widt...  75.1 us

profile of v1, /device:TPU:0, one launch (start us, length us, event | category | flops | bytes accessed | tf_op | source)
XLA Modules:
  0.0 280.1 jit_solution(2509175435633175660)
XLA Ops:
  0.0 204.9 %shard_map.28 = (bf16[24,1024,256]{2,1,0:T(8,128)(2,1)}, bf16[2048,8192]{1,0:T(8,128)(2,1)}, bf16[1024,4096]{1,0:T(8,128)(2,1)}, f32[2,1024,8192]{2,1,0:T(8,128)}) custom-call(bf16[5120,1280]{1,0:T(8,128)(2,1)} %l_ref.3, bf16[5,2,512,8192]{3,2,1,0:T(8,128)(2,1)} %bitcast.1.b_ref), custom_call_target="tpu_custom_call" | custom-call | tf_op jit(solution)/shard_map/pallas_call | solution.py:400
  204.9 75.1 %shard_map.29 = bf16[5120,8192]{1,0:T(8,128)(2,1)} custom-call(bf16[5120,1280]{1,0:T(8,128)(2,1)} %l_ref.3, bf16[20,256,8192]{2,1,0:T(8,128)(2,1)} %bitcast.b_ref, bf16[24,1024,256]{2,1,0:T(8,128)(2,1)} %get-tuple-element.8.lg_ref, bf16[2048,8192]{1,0:T(8,128)(2,1)} %get-tuple-element.9.x1_ref, bf16[1024,4096]{1,0:T(8,128)(2,1)} %get-tuple-element.10.x2_ref), custom_call_target="tpu_custom_call" | custom-call | tf_op jit(solution)/shard_map/pallas_call | solution.py:420

commit v2 on v1

--- a/solution.py
+++ b/solution.py
@@ -13,8 +13,12 @@
 SUP = 4 * BLK
 TN = 512
 NSUP = 5
-NT = 16
-NT2 = 8
+WIDE = 1024
+DN = 512
+NT = 8
+NT2 = 2
+N0 = NT2 * WIDE // TN
+N1 = (NT - NT2) * WIDE // TN
 ROWS = (0, 1, 2, 3)
 
 CHUNKS = [(s, t) for s in (4, 3, 2, 1, 0) for t in range(s + 1)]
@@ -74,7 +78,11 @@
     return pl.ds(j * TN, TN) if isinstance(j, int) else pl.ds(pl.multiple_of(j * TN, TN), TN)
 
 
-def gather_kernel(l_ref, b_ref, lg_ref, x1_ref, x2_ref, pf_ref, la, lb, lc, bbuf, pbuf, obuf, own_sem, dsend, drecv, xsend, xrecv,
+def wide(j):
+    return pl.ds(pl.multiple_of(j * WIDE, WIDE), WIDE)
+
+
+def gather_kernel(l_ref, b_ref, lg_ref, x1_ref, x2_ref, pf_ref, la, lb, lc, bbuf, pbuf, pin, obuf, own_sem, dsend, drecv, xsend, xrecv,
                   fsend, frecv, bsem, psem, osem, gsem):
     me = lax.axis_index("col")
     core = lax.rem(me, 2)
@@ -135,137 +143,186 @@
         from_oth(s, t).wait_recv()
         forward(s, t).start()
 
-    jobs = [(4, "part", NT), (3, "part", NT), (4, "rest", NT), (3, "rest", NT), (2, "all", NT2)]
-    passes = {"part": lambda s: 2 * s * 512, "rest": lambda s: 2 * s * 512 + 1280, "all": lambda s: 4 * s * 512 + 1280}
-    events = [dict() for _ in jobs]
-    clock, todo = 6.0, list(enumerate(CHUNKS))
-    for q, (s, kind, n) in enumerate(jobs):
+    jobs = [((4, 3), "part", NT), ((4,), "rest", NT), ((3,), "rest", NT), ((2,), "all", NT2)]
+    cycles = {"part": lambda s: 2 * s * 512, "rest": lambda s: 2 * s * 512 + 1280, "all": lambda s: 4 * s * 512 + 1280}
+    events, forced = [[] for _ in jobs], [[] for _ in jobs]
+    clock, todo = 5.0, list(enumerate(CHUNKS))
+    for q, (sups, kind, n) in enumerate(jobs):
+        while kind != "part" and todo and todo[0][1][0] >= sups[0]:
+            i, st = todo.pop(0)
+            clock = max(clock, 5.0 + 11.3 * (i + 1))
+            forced[q].append(st)
         for j in range(n):
-            if todo and clock > 5.0 + 11.3 * (todo[0][0] + 1) + 1.5:
-                events[q][j] = todo.pop(0)[1]
-            clock += passes[kind](s) / 1850.0
+            while todo and clock > 5.0 + 11.3 * (todo[0][0] + 1) + 1.0:
+                events[q].append((j, todo.pop(0)[1]))
+            clock += 2 * sum(map(cycles[kind], sups)) / 1850.0
     left = [st for _, st in todo]
 
     def b_copies(q, j, slot):
-        s, kind, _ = jobs[q]
+        s, kind = jobs[q][0][0], jobs[q][1]
         dst = bbuf.at[slot]
         if kind == "part":
-            return [pltpu.make_async_copy(b_ref.at[0:s, chip, :, cols(j)], dst.at[0:s], bsem.at[slot, 0])]
-        far = pltpu.make_async_copy(b_ref.at[0:s, 1 - chip, :, cols(j)], dst.at[0:s], bsem.at[slot, 0])
+            return [pltpu.make_async_copy(b_ref.at[0:s, chip, :, wide(j)], dst.at[0:s], bsem.at[slot, 0])]
+        far = pltpu.make_async_copy(b_ref.at[0:s, 1 - chip, :, wide(j)], dst.at[0:s], bsem.at[slot, 0])
         if kind == "rest":
-            return [far, pltpu.make_async_copy(b_ref.at[s, :, :, cols(j)], dst.at[pl.ds(s, 2)], bsem.at[slot, 1])]
+            return [far, pltpu.make_async_copy(b_ref.at[s, :, :, wide(j)], dst.at[pl.ds(s, 2)], bsem.at[slot, 1])]
         return [
-            pltpu.make_async_copy(b_ref.at[0:s, chip, :, cols(j)], dst.at[0:s], bsem.at[slot, 0]),
-            pltpu.make_async_copy(b_ref.at[0:s, 1 - chip, :, cols(j)], dst.at[pl.ds(s, s)], bsem.at[slot, 2]),
-            pltpu.make_async_copy(b_ref.at[s, :, :, cols(j)], dst.at[pl.ds(2 * s, 2)], bsem.at[slot, 1]),
+            pltpu.make_async_copy(b_ref.at[0:s, chip, :, wide(j)], dst.at[0:s], bsem.at[slot, 0]),
+            pltpu.make_async_copy(b_ref.at[0:s, 1 - chip, :, wide(j)], dst.at[pl.ds(s, s)], bsem.at[slot, 2]),
+            pltpu.make_async_copy(b_ref.at[s, :, :, wide(j)], dst.at[pl.ds(2 * s, 2)], bsem.at[slot, 1]),
         ]
 
     def run_job(q):
-        s, kind, n = jobs[q]
-        lbuf = strips[s]
+        sups, kind, n = jobs[q]
         nxt = q + 1 if q + 1 < len(jobs) else None
 
         def start_b(qq, j, slot):
             for c in b_copies(qq, j, slot):
                 c.start()
 
-        def out_copy(j):
-            slot = j & 1
-            if kind == "part":
-                return pltpu.make_async_copy(pbuf.at[slot], pf_ref.at[s - 3, :, cols(j)], osem.at[slot])
-            if kind == "rest":
-                return pltpu.make_async_copy(obuf.at[slot], x1_ref.at[pl.ds(SUP * (s - 3), SUP), cols(j)], osem.at[slot])
-            return pltpu.make_async_copy(obuf.at[slot], x2_ref.at[:, cols(j)], osem.at[slot])
-
-        def part_copy(j):
-            slot = j & 1
-            return pltpu.make_async_copy(pf_ref.at[s - 3, :, cols(j)], pbuf.at[slot], psem.at[slot])
+        def x_copy(qq, j):
+            (ss, *_), kk, _ = jobs[qq]
+            dst = x1_ref.at[pl.ds(SUP * (ss - 3), SUP), wide(j)] if kk == "rest" else x2_ref.at[:, wide(j)]
+            return pltpu.make_async_copy(obuf.at[j & 1], dst, osem.at[j & 1])
+
+        def pf_out(i, j):
+            return pltpu.make_async_copy(pbuf.at[i], pf_ref.at[1 - i, :, wide(j)], gsem.at[i])
+
+        def part_copy(qq, j):
+            return pltpu.make_async_copy(pf_ref.at[jobs[qq][0][0] - 3, :, wide(j)], pin.at[j & 1], psem.at[j & 1])
 
         def body(j, carry):
             slot = j & 1
-            pl.when(j < n - 1)(lambda: start_b(q, j + 1, 1 - slot))
+
+            @pl.when(j < n - 1)
+            def _():
+                start_b(q, j + 1, 1 - slot)
+                if kind == "rest":
+                    part_copy(q, j + 1).start()
+
             if nxt is not None:
-                pl.when(j == n - 1)(lambda: start_b(nxt, 0, 0))
+
+                @pl.when(j == n - 1)
+                def _():
+                    start_b(nxt, 0, 0)
+                    if jobs[nxt][1] == "rest":
+                        part_copy(nxt, 0).start()
+
             if events[q]:
-                hit = functools.reduce(jnp.logical_or, [j == jj for jj in events[q]])
+                hit = functools.reduce(jnp.logical_or, [j == jj for jj, _ in events[q]])
 
                 @pl.when(hit)
                 def _():
-                    for jj, st in events[q].items():
+                    for jj, st in events[q]:
                         pl.when(j == jj)(functools.partial(pass_on, *st))
 
-            pl.when(j >= 1)(lambda: out_copy(j - 1).start())
-            pl.when(j >= 2)(lambda: out_copy(j - 2).wait())
+            if kind == "part":
+                pl.when(j >= 1)(lambda: pf_out(1, j - 1).start())
+            else:
+
+                @pl.when(j == 0)
+                def _():
+                    if q == 1:
+                        pf_out(1, NT - 1).start()
+                        pf_out(0, NT - 1).wait()
+                    else:
+                        x_copy(q - 1, jobs[q - 1][2] - 1).start()
+                        x_copy(q - 1, jobs[q - 1][2] - 2).wait()
+
+                @pl.when(j == 1)
+                def _():
+                    x_copy(q, 0).start()
+                    if q == 1:
+                        pf_out(1, NT - 1).wait()
+                    else:
+                        x_copy(q - 1, jobs[q - 1][2] - 1).wait()
+
+                @pl.when(j >= 2)
+                def _():
+                    x_copy(q, j - 1).start()
+                    x_copy(q, j - 2).wait()
+
             if kind == "rest":
-                pl.when(j < n - 1)(lambda: part_copy(j + 1).start())
-                part_copy(j).wait()
+                part_copy(q, j).wait()
             for c in b_copies(q, j, slot):
                 c.wait()
-            base = 0 if kind == "part" else (2 * s if kind == "rest" else 0)
-            for r in ROWS:
-                rows = slice(r * BLK, (r + 1) * BLK)
-                n_k = 2 * s if kind == "part" else (4 * s + r + 1 - base)
-                rhs = bbuf[slot, 0:(n_k + 1) // 2].reshape(-1, TN)[0:n_k * BLK]
-                v = jnp.dot(lbuf[rows, base * BLK:(base + n_k) * BLK], rhs, preferred_element_type=F32)
+            for i, s in enumerate(sups):
                 if kind == "part":
-                    pbuf[slot, rows, :] = v
-                elif kind == "rest":
-                    obuf[slot, rows, :] = (v + pbuf[slot, rows, :]).astype(BF)
-                else:
-                    obuf[slot, rows, :] = v.astype(BF)
+                    pl.when(j >= 1)(lambda: pf_out(i, j - 1).wait())
+                    if i == 1:
+
+                        @pl.when(j == 0)
+                        def _():
+                            for t in range(3):
+                                own_copy(3, t).wait()
+                                from_sib(3, t).wait_recv()
+
+                base = 2 * s if kind == "rest" else 0
+                for r in ROWS:
+                    rows = slice(r * BLK, (r + 1) * BLK)
+                    n_k = 2 * s if kind == "part" else 4 * s + r + 1 - base
+                    for h in range(WIDE // DN):
+                        half = slice(h * DN, (h + 1) * DN)
+                        rhs = bbuf[slot, 0:(n_k + 1) // 2, :, half].reshape(-1, DN)[0:n_k * BLK]
+                        v = jnp.dot(strips[s][rows, base * BLK:(base + n_k) * BLK], rhs, preferred_element_type=F32)
+                        if kind == "part":
+                            pbuf[i, rows, half] = v
+                        elif kind == "rest":
+                            obuf[slot, rows, half] = (v + pin[slot, rows, half]).astype(BF)
+                        else:
+                            obuf[slot, rows, half] = v.astype(BF)
+                    if kind == "part" and (i, r) == (1, 0):
+                        pf_out(0, j).start()
             return carry
 
-        if kind == "rest":
-            part_copy(0).start()
         lax.fori_loop(0, n, body, 0)
-        out_copy(n - 1).start()
-        out_copy(n - 2).wait()
-        out_copy(n - 1).wait()
+        if nxt is None:
+            x_copy(q, n - 1).start()
+            x_copy(q, n - 2).wait()
+            x_copy(q, n - 1).wait()
 
     def inner():
-        for s in (4, 3, 2):
-            for t in range(s + 1):
-                own_copy(s, t).start()
         for c in b_copies(0, 0, 0):
             c.start()
+        early = [(4, t) for t in range(4)] + [(3, t) for t in range(3)]
+        for st in early:
+            own_copy(*st).start()
         barrier = pltpu.get_barrier_semaphore()
         for dev in (sib, oth):
             pl.semaphore_signal(barrier, inc=1, device_id={"col": dev}, device_id_type=pl.DeviceIdType.MESH)
         pl.semaphore_wait(barrier, 2)
-        for t in range(5):
-            to_sib(4, t).start()
-        for s, t in CHUNKS:
-            to_oth(s, t).start()
-        for s, t in CHUNKS[5:]:
-            to_sib(s, t).start()
-
-        for s, t in CHUNKS[:12]:
-            own_copy(s, t).wait()
+        for st in early:
+            to_sib(*st).start()
+        for st in CHUNKS:
+            to_oth(*st).start()
+        for st in CHUNKS:
+            if st not in early:
+                to_sib(*st).start()
+                if st[0] >= 2:
+                    own_copy(*st).start()
+
         for t in range(4):
+            own_copy(4, t).wait()
             from_sib(4, t).wait_recv()
         run_job(0)
-        for t in range(3):
-            from_sib(3, t).wait_recv()
-        run_job(1)
-        from_sib(4, 4).wait_recv()
-        for t in range(5):
-            from_fwd(4, t).wait_recv()
-        run_job(2)
-        from_sib(3, 3).wait_recv()
-        for t in range(4):
-            from_fwd(3, t).wait_recv()
-        run_job(3)
-        for t in range(3):
-            from_sib(2, t).wait_recv()
-            from_fwd(2, t).wait_recv()
+        for q, s in ((1, 4), (2, 3), (3, 2)):
+            for st in forced[q]:
+                pass_on(*st)
+            for t in range(s + 1):
+                if t == s or s == 2:
+                    own_copy(s, t).wait()
+                    from_sib(s, t).wait_recv()
+                from_fwd(s, t).wait_recv()
+            if s > 2:
+                run_job(q)
         saves = []
         for k in range(12):
             t, u = k % 4 // 2, k % 2
             kb = k if k >= 8 else 4 * t + 2 * (chip if k < 4 else 1 - chip) + u
-            saves.append(pltpu.make_async_copy(lc.at[:, pl.ds(k * BLK, BLK)], lg_ref.at[LG_BASE[2] + kb], gsem.at[k]))
+            saves.append(pltpu.make_async_copy(lc.at[:, pl.ds(k * BLK, BLK)], lg_ref.at[LG_BASE[2] + kb], gsem.at[2 + k]))
         for c in saves:
             c.start()
-        run_job(4)
+        run_job(3)
         for s, t in left:
             pass_on(s, t)
         for c in saves:
@@ -284,7 +341,7 @@
 
 def finish_kernel(l_ref, b_ref, lg_ref, x1_ref, x2_ref, x_ref, lbuf, bbuf, obuf, cbuf, dbuf, lsem, bsem, osem, csem, dsem):
     me = lax.axis_index("col")
-    jobs = [(0, NT2, (0, 1)), (NT2, NT - NT2, (0, 1, 2))]
+    jobs = [(0, N0, (0, 1)), (N0, N1, (0, 1, 2))]
 
     def l_copies(s):
         base = LG_BASE[s]
@@ -312,16 +369,18 @@
             return pltpu.make_async_copy(obuf.at[slot, u], x_ref.at[pl.ds(SUP * sups[u], SUP), cols(first + j)], osem.at[slot, u])
 
         if q == 0:
-            rows = SUP // n
+            chunks = n
+            rows = SUP // chunks
 
             def c_in(j):
                 return pltpu.make_async_copy(x2_ref.at[pl.ds(pl.multiple_of(j * rows, rows), rows), :], dbuf.at[j & 1], dsem.at[0, j & 1])
 
             def c_out(j):
                 return pltpu.make_async_copy(
-                    dbuf.at[j & 1], x_ref.at[pl.ds(pl.multiple_of(2 * SUP + j * rows, rows), rows), pl.ds(0, NT2 * TN)], dsem.at[1, j & 1])
+                    dbuf.at[j & 1], x_ref.at[pl.ds(pl.multiple_of(2 * SUP + j * rows, rows), rows), pl.ds(0, N0 * TN)], dsem.at[1, j & 1])
         else:
-            rows = 2 * SUP // n
+            chunks = 8
+            rows = 2 * SUP // chunks
 
             def c_in(j):
                 return pltpu.make_async_copy(x1_ref.at[pl.ds(pl.multiple_of(j * rows, rows), rows), :], cbuf.at[j & 1], csem.at[0, j & 1])
@@ -348,10 +407,15 @@
                     when(True if last else j >= 1, lambda: out_copy(u, j - 1).start())
                     when(True if last else j >= 2, lambda: out_copy(u, j - 2).wait())
             if not last:
-                pl.when(j >= 1)(lambda: c_out(j - 1).wait())
-                c_in(j + 1).start()
-            when(True if last else j >= 0, lambda: c_in(j).wait())
-            when(True if last else j >= 0, lambda: c_out(j).start())
+                pl.when(jnp.logical_and(j >= 1, j <= chunks))(lambda: c_out(j - 1).wait())
+                pl.when(j + 1 < chunks)(lambda: c_in(j + 1).start())
+            if not last or j < chunks:
+
+                def move():
+                    c_in(j).wait()
+                    c_out(j).start()
+
+                when(True if last else jnp.logical_and(j >= 0, j < chunks), move)
 
         def lhs_of(u, k, r):
             return lbuf[LG_BASE[sups[u]] + k, r * BLK:(r + 1) * BLK, :]
@@ -365,8 +429,9 @@
         subs = [diag_passes(4 * s) + [(4 * s, ROWS)] + [(k, ROWS) for k in range(4 * s)] for s in sups]
         run_tiles(accs, subs, lhs_of, rhs_of, emit, top, n)
         out_copy(lasts, n - 1).start()
-        c_out(n - 2).wait()
-        c_out(n - 1).wait()
+        if chunks == n:
+            c_out(n - 2).wait()
+            c_out(n - 1).wait()
         for u in range(len(sups)):
             if u == lasts:
                 out_copy(u, n - 2).wait()
@@ -402,7 +467,7 @@
             out_shape=(
                 jax.ShapeDtypeStruct((24, SUP, BLK), BF),
                 jax.ShapeDtypeStruct((2 * SUP, width), BF),
-                jax.ShapeDtypeStruct((SUP, NT2 * TN), BF),
+                jax.ShapeDtypeStruct((SUP, N0 * TN), BF),
                 jax.ShapeDtypeStruct((2, SUP, width), F32),
             ),
             in_specs=[hbm] * 2,
@@ -411,10 +476,11 @@
                 pltpu.VMEM((SUP, 20 * BLK), BF),
                 pltpu.VMEM((SUP, 16 * BLK), BF),
                 pltpu.VMEM((SUP, 12 * BLK), BF),
-                pltpu.VMEM((2, 6, 2 * BLK, TN), BF),
-                pltpu.VMEM((2, SUP, TN), F32),
-                pltpu.VMEM((2, SUP, TN), BF),
-            ] + [dma((15,))] * 7 + [dma((2, 3)), dma((2,)), dma((2,)), dma((12,))],
+                pltpu.VMEM((2, 6, 2 * BLK, WIDE), BF),
+                pltpu.VMEM((2, SUP, WIDE), F32),
+                pltpu.VMEM((2, SUP, WIDE), F32),
+                pltpu.VMEM((2, SUP, WIDE), BF),
+            ] + [dma((15,))] * 7 + [dma((2, 3)), dma((2,)), dma((2,)), dma((14,))],
             compiler_params=pltpu.CompilerParams(vmem_limit_bytes=62 * 1024 * 1024, collective_id=0, has_side_effects=True),
         )(l_cols, b4)
         return pl.pallas_call(
@@ -426,8 +492,8 @@
                 pltpu.VMEM((24, SUP, BLK), BF),
                 pltpu.VMEM((2, 12, BLK, TN), BF),
                 pltpu.VMEM((2, 3, SUP, TN), BF),
-                pltpu.VMEM((2, 2 * SUP // (NT - NT2), width), BF),
-                pltpu.VMEM((2, SUP // NT2, NT2 * TN), BF),
+                pltpu.VMEM((2, 2 * SUP // 8, width), BF),
+                pltpu.VMEM((2, SUP // N0, N0 * TN), BF),
             ] + [dma((24,)), dma((2,)), dma((2, 3)), dma((2, 2)), dma((2, 2))],
             compiler_params=pltpu.CompilerParams(vmem_limit_bytes=62 * 1024 * 1024),
         )(l_cols, b3, lg, x1, x2)

time: 281 us -> 261 us (0.929)
  Pallas kernels: 280 us -> 261 us
    pallas_call x1, Pallas kernels: 205 us -> 177 us  [local_product(): pl.pallas_call(gather_kernel, out_shape=(jax.ShapeDtypeStruct((24, SUP, B...]
    pallas_call x1, Pallas kernels: 75.1 us -> 83.9 us  [local_product(): pl.pallas_call(finish_kernel, out_shape=jax.ShapeDtypeStruct((order, widt...]
where the time goes in v2:
time: 261 us
  Pallas kernels  261 us (100%)
    pallas_call x1, Pallas kernels, local_product(): pl.pallas_call(gather_kernel, out_shape=(jax.ShapeDtypeStruct((24, SUP, B...  177 us
    pallas_call x1, Pallas kernels, local_product(): pl.pallas_call(finish_kernel, out_shape=jax.ShapeDtypeStruct((order, widt...  83.9 us

profile of v2, /device:TPU:0, one launch (start us, length us, event | category | flops | bytes accessed | tf_op | source)
XLA Modules:
  0.0 260.8 jit_solution(157241331012074787)
XLA Ops:
  0.0 176.7 %shard_map.28 = (bf16[24,1024,256]{2,1,0:T(8,128)(2,1)}, bf16[2048,8192]{1,0:T(8,128)(2,1)}, bf16[1024,2048]{1,0:T(8,128)(2,1)}, f32[2,1024,8192]{2,1,0:T(8,128)}) custom-call(bf16[5120,1280]{1,0:T(8,128)(2,1)} %l_ref.3, bf16[5,2,512,8192]{3,2,1,0:T(8,128)(2,1)} %bitcast.1.b_ref), custom_call_target="tpu_custom_call" | custom-call | tf_op jit(solution)/shard_map/pallas_call | solution.py:465
  176.7 83.9 %shard_map.29 = bf16[5120,8192]{1,0:T(8,128)(2,1)} custom-call(bf16[5120,1280]{1,0:T(8,128)(2,1)} %l_ref.3, bf16[20,256,8192]{2,1,0:T(8,128)(2,1)} %bitcast.b_ref, bf16[24,1024,256]{2,1,0:T(8,128)(2,1)} %get-tuple-element.8.lg_ref, bf16[2048,8192]{1,0:T(8,128)(2,1)} %get-tuple-element.9.x1_ref, bf16[1024,2048]{1,0:T(8,128)(2,1)} %get-tuple-element.10.x2_ref), custom_call_target="tpu_custom_call" | custom-call | tf_op jit(solution)/shard_map/pallas_call | solution.py:486

commit v3 on v2

--- a/solution.py
+++ b/solution.py
@@ -19,6 +19,7 @@
 NT2 = 2
 N0 = NT2 * WIDE // TN
 N1 = (NT - NT2) * WIDE // TN
+COPY = -(-2 * SUP // N1 // 16) * 16
 ROWS = (0, 1, 2, 3)
 
 CHUNKS = [(s, t) for s in (4, 3, 2, 1, 0) for t in range(s + 1)]
@@ -83,7 +84,7 @@
 
 
 def gather_kernel(l_ref, b_ref, lg_ref, x1_ref, x2_ref, pf_ref, la, lb, lc, bbuf, pbuf, pin, obuf, own_sem, dsend, drecv, xsend, xrecv,
-                  fsend, frecv, bsem, psem, osem, gsem):
+                  ysend, yrecv, fsend, frecv, bsem, psem, osem, gsem):
     me = lax.axis_index("col")
     core = lax.rem(me, 2)
     chip = me // 2
@@ -115,9 +116,18 @@
         i = CHUNK_ID[s, t]
         return remote(own_src(s, t), place(s, t, me, False), dsend.at[i], drecv.at[i], sib)
 
-    def to_oth(s, t):
+    def cross(s, t, dev, do):
         i = CHUNK_ID[s, t]
-        return remote(own_src(s, t), place(s, t, me, True), xsend.at[i], xrecv.at[i], oth)
+        if t < s:
+            do(remote(own_src(s, t), place(s, t, dev, True), xsend.at[i], xrecv.at[i], oth))
+            return
+        for r in ROWS:
+
+            @pl.when(r >= dev)
+            def _():
+                src = l_ref.at[pl.ds(SUP * s + BLK * r, BLK), pl.ds(BLK * t, BLK)]
+                dst = place(s, t, dev, True).at[pl.ds(BLK * r, BLK)]
+                do(remote(src, dst, ysend.at[s, r], yrecv.at[s, r], oth))
 
     def forward(s, t):
         i = CHUNK_ID[s, t]
@@ -129,37 +139,34 @@
         here = place(s, t, sib, False)
         return remote(here, here, dsend.at[i], drecv.at[i], sib)
 
-    def from_oth(s, t):
-        i = CHUNK_ID[s, t]
-        here = place(s, t, oth, True)
-        return remote(here, here, xsend.at[i], xrecv.at[i], oth)
-
     def from_fwd(s, t):
         i = CHUNK_ID[s, t]
         here = place(s, t, sib_oth, True)
         return remote(here, here, fsend.at[i], frecv.at[i], sib)
 
     def pass_on(s, t):
-        from_oth(s, t).wait_recv()
+        cross(s, t, oth, lambda c: c.wait_recv())
         forward(s, t).start()
 
-    jobs = [((4, 3), "part", NT), ((4,), "rest", NT), ((3,), "rest", NT), ((2,), "all", NT2)]
+    jobs = [((3, 4), "part", NT), ((4,), "rest", NT), ((3,), "rest", NT), ((2,), "all", NT2)]
     cycles = {"part": lambda s: 2 * s * 512, "rest": lambda s: 2 * s * 512 + 1280, "all": lambda s: 4 * s * 512 + 1280}
     events, forced = [[] for _ in jobs], [[] for _ in jobs]
-    clock, todo = 5.0, list(enumerate(CHUNKS))
+    clock, due, todo = 5.0, 4.0, []
+    for s, t in CHUNKS:
+        due += 11.3 if t < s else 9.9
+        todo.append((due, (s, t)))
     for q, (sups, kind, n) in enumerate(jobs):
         while kind != "part" and todo and todo[0][1][0] >= sups[0]:
-            i, st = todo.pop(0)
-            clock = max(clock, 5.0 + 11.3 * (i + 1))
-            forced[q].append(st)
+            clock = max(clock, todo[0][0])
+            forced[q].append(todo.pop(0)[1])
         for j in range(n):
-            while todo and clock > 5.0 + 11.3 * (todo[0][0] + 1) + 1.0:
+            while todo and clock > todo[0][0] + 1.5:
                 events[q].append((j, todo.pop(0)[1]))
             clock += 2 * sum(map(cycles[kind], sups)) / 1850.0
     left = [st for _, st in todo]
 
     def b_copies(q, j, slot):
-        s, kind = jobs[q][0][0], jobs[q][1]
+        s, kind = jobs[q][0][-1], jobs[q][1]
         dst = bbuf.at[slot]
         if kind == "part":
             return [pltpu.make_async_copy(b_ref.at[0:s, chip, :, wide(j)], dst.at[0:s], bsem.at[slot, 0])]
@@ -186,7 +193,7 @@
             return pltpu.make_async_copy(obuf.at[j & 1], dst, osem.at[j & 1])
 
         def pf_out(i, j):
-            return pltpu.make_async_copy(pbuf.at[i], pf_ref.at[1 - i, :, wide(j)], gsem.at[i])
+            return pltpu.make_async_copy(pbuf.at[i], pf_ref.at[i, :, wide(j)], gsem.at[i])
 
         def part_copy(qq, j):
             return pltpu.make_async_copy(pf_ref.at[jobs[qq][0][0] - 3, :, wide(j)], pin.at[j & 1], psem.at[j & 1])
@@ -253,9 +260,9 @@
 
                         @pl.when(j == 0)
                         def _():
-                            for t in range(3):
-                                own_copy(3, t).wait()
-                                from_sib(3, t).wait_recv()
+                            for t in range(4):
+                                own_copy(4, t).wait()
+                                from_sib(4, t).wait_recv()
 
                 base = 2 * s if kind == "rest" else 0
                 for r in ROWS:
@@ -273,19 +280,31 @@
                             obuf[slot, rows, half] = v.astype(BF)
                     if kind == "part" and (i, r) == (1, 0):
                         pf_out(0, j).start()
+                    if kind == "all" and r == 2:
+
+                        @pl.when(j == n - 1)
+                        def _():
+                            for st in left:
+                                pass_on(*st)
+
             return carry
 
         lax.fori_loop(0, n, body, 0)
         if nxt is None:
             x_copy(q, n - 1).start()
-            x_copy(q, n - 2).wait()
+            if n > 1:
+                x_copy(q, n - 2).wait()
+            else:
+                x_copy(q - 1, jobs[q - 1][2] - 1).wait()
             x_copy(q, n - 1).wait()
 
     def inner():
+        early = [(3, t) for t in range(3)] + [(4, t) for t in range(4)]
+        for st in early[:3]:
+            own_copy(*st).start()
         for c in b_copies(0, 0, 0):
             c.start()
-        early = [(4, t) for t in range(4)] + [(3, t) for t in range(3)]
-        for st in early:
+        for st in early[3:]:
             own_copy(*st).start()
         barrier = pltpu.get_barrier_semaphore()
         for dev in (sib, oth):
@@ -294,16 +313,16 @@
         for st in early:
             to_sib(*st).start()
         for st in CHUNKS:
-            to_oth(*st).start()
+            cross(*st, me, lambda c: c.start())
         for st in CHUNKS:
             if st not in early:
                 to_sib(*st).start()
                 if st[0] >= 2:
                     own_copy(*st).start()
 
-        for t in range(4):
-            own_copy(4, t).wait()
-            from_sib(4, t).wait_recv()
+        for t in range(3):
+            own_copy(3, t).wait()
+            from_sib(3, t).wait_recv()
         run_job(0)
         for q, s in ((1, 4), (2, 3), (3, 2)):
             for st in forced[q]:
@@ -323,8 +342,6 @@
         for c in saves:
             c.start()
         run_job(3)
-        for s, t in left:
-            pass_on(s, t)
         for c in saves:
             c.wait()
         for s in (1, 0):
@@ -333,7 +350,7 @@
                 from_fwd(s, t).wait_recv()
         for s, t in CHUNKS:
             to_sib(s, t).wait_send()
-            to_oth(s, t).wait_send()
+            cross(s, t, me, lambda c: c.wait_send())
             forward(s, t).wait_send()
 
     inner()
@@ -379,15 +396,18 @@
                 return pltpu.make_async_copy(
                     dbuf.at[j & 1], x_ref.at[pl.ds(pl.multiple_of(2 * SUP + j * rows, rows), rows), pl.ds(0, N0 * TN)], dsem.at[1, j & 1])
         else:
-            chunks = 8
-            rows = 2 * SUP // chunks
+            chunks = n
+            rows = COPY
+
+            def part(j):
+                return pl.multiple_of(jnp.minimum(j * rows, 2 * SUP - rows), 16)
 
             def c_in(j):
-                return pltpu.make_async_copy(x1_ref.at[pl.ds(pl.multiple_of(j * rows, rows), rows), :], cbuf.at[j & 1], csem.at[0, j & 1])
+                return pltpu.make_async_copy(x1_ref.at[pl.ds(part(j), rows), :], cbuf.at[j & 1], csem.at[0, j & 1])
 
             def c_out(j):
                 return pltpu.make_async_copy(
-                    cbuf.at[j & 1], x_ref.at[pl.ds(pl.multiple_of(3 * SUP + j * rows, rows), rows), :], csem.at[1, j & 1])
+                    cbuf.at[j & 1], x_ref.at[pl.ds(3 * SUP + part(j), rows), :], csem.at[1, j & 1])
 
         def top(j):
             last = isinstance(j, int)
@@ -440,12 +460,14 @@
     def inner(*refs):
         accs = (refs[:4], refs[4:])
         b_copy(0, 0, 0).start()
-        for s in (0, 1, 2):
+        for s in (0, 1):
             for c in l_copies(s):
                 c.start()
         for s in (0, 1):
             for c in l_copies(s):
                 c.wait()
+        for c in l_copies(2):
+            c.start()
         run_job(0, accs)
         for c in l_copies(2):
             c.wait()
@@ -480,7 +502,7 @@
                 pltpu.VMEM((2, SUP, WIDE), F32),
                 pltpu.VMEM((2, SUP, WIDE), F32),
                 pltpu.VMEM((2, SUP, WIDE), BF),
-            ] + [dma((15,))] * 7 + [dma((2, 3)), dma((2,)), dma((2,)), dma((14,))],
+            ] + [dma((15,))] * 5 + [dma((5, 4))] * 2 + [dma((15,))] * 2 + [dma((2, 3)), dma((2,)), dma((2,)), dma((14,))],
             compiler_params=pltpu.CompilerParams(vmem_limit_bytes=62 * 1024 * 1024, collective_id=0, has_side_effects=True),
         )(l_cols, b4)
         return pl.pallas_call(
@@ -492,7 +514,7 @@
                 pltpu.VMEM((24, SUP, BLK), BF),
                 pltpu.VMEM((2, 12, BLK, TN), BF),
                 pltpu.VMEM((2, 3, SUP, TN), BF),
-                pltpu.VMEM((2, 2 * SUP // 8, width), BF),
+                pltpu.VMEM((2, COPY, width), BF),
                 pltpu.VMEM((2, SUP // N0, N0 * TN), BF),
             ] + [dma((24,)), dma((2,)), dma((2, 3)), dma((2, 2)), dma((2, 2))],
             compiler_params=pltpu.CompilerParams(vmem_limit_bytes=62 * 1024 * 1024),

time: 261 us -> 257 us (0.985)
  Pallas kernels: 261 us -> 257 us
    pallas_call x1, Pallas kernels: 177 us -> 173 us  [local_product(): pl.pallas_call(gather_kernel, out_shape=(jax.ShapeDtypeStruct((24, SUP, B...]
where the time goes in v3:
time: 257 us
  Pallas kernels  257 us (100%)
    pallas_call x1, Pallas kernels, local_product(): pl.pallas_call(gather_kernel, out_shape=(jax.ShapeDtypeStruct((24, SUP, B...  173 us
    pallas_call x1, Pallas kernels, local_product(): pl.pallas_call(finish_kernel, out_shape=jax.ShapeDtypeStruct((order, widt...  83.9 us

profile of v3, /device:TPU:0, one launch (start us, length us, event | category | flops | bytes accessed | tf_op | source)
XLA Modules:
  0.0 257.1 jit_solution(2587868636338989206)
XLA Ops:
  0.0 173.0 %shard_map.28 = (bf16[24,1024,256]{2,1,0:T(8,128)(2,1)}, bf16[2048,8192]{1,0:T(8,128)(2,1)}, bf16[1024,2048]{1,0:T(8,128)(2,1)}, f32[2,1024,8192]{2,1,0:T(8,128)}) custom-call(bf16[5120,1280]{1,0:T(8,128)(2,1)} %l_ref.3, bf16[5,2,512,8192]{3,2,1,0:T(8,128)(2,1)} %bitcast.1.b_ref), custom_call_target="tpu_custom_call" | custom-call | tf_op jit(solution)/shard_map/pallas_call | solution.py:487
  173.0 83.9 %shard_map.29 = bf16[5120,8192]{1,0:T(8,128)(2,1)} custom-call(bf16[5120,1280]{1,0:T(8,128)(2,1)} %l_ref.3, bf16[20,256,8192]{2,1,0:T(8,128)(2,1)} %bitcast.b_ref, bf16[24,1024,256]{2,1,0:T(8,128)(2,1)} %get-tuple-element.8.lg_ref, bf16[2048,8192]{1,0:T(8,128)(2,1)} %get-tuple-element.9.x1_ref, bf16[1024,2048]{1,0:T(8,128)(2,1)} %get-tuple-element.10.x2_ref), custom_call_target="tpu_custom_call" | custom-call | tf_op jit(solution)/shard_map/pallas_call | solution.py:508

commit v4 on v3

--- a/solution.py
+++ b/solution.py
@@ -151,7 +151,7 @@
     jobs = [((3, 4), "part", NT), ((4,), "rest", NT), ((3,), "rest", NT), ((2,), "all", NT2)]
     cycles = {"part": lambda s: 2 * s * 512, "rest": lambda s: 2 * s * 512 + 1280, "all": lambda s: 4 * s * 512 + 1280}
     events, forced = [[] for _ in jobs], [[] for _ in jobs]
-    clock, due, todo = 5.0, 4.0, []
+    clock, due, todo = 5.0, 3.5, []
     for s, t in CHUNKS:
         due += 11.3 if t < s else 9.9
         todo.append((due, (s, t)))
@@ -160,7 +160,7 @@
             clock = max(clock, todo[0][0])
             forced[q].append(todo.pop(0)[1])
         for j in range(n):
-            while todo and clock > todo[0][0] + 1.5:
+            while todo and clock > todo[0][0] + 0.3:
                 events[q].append((j, todo.pop(0)[1]))
             clock += 2 * sum(map(cycles[kind], sups)) / 1850.0
     left = [st for _, st in todo]

time: 257 us -> 255 us (level)
  no operation moved by 1% of the time
where the time goes in v4:
time: 255 us
  Pallas kernels  255 us (100%)
    pallas_call x1, Pallas kernels, local_product(): pl.pallas_call(gather_kernel, out_shape=(jax.ShapeDtypeStruct((24, SUP, B...  171 us
    pallas_call x1, Pallas kernels, local_product(): pl.pallas_call(finish_kernel, out_shape=jax.ShapeDtypeStruct((order, widt...  83.9 us

profile of v4, /device:TPU:0, one launch (start us, length us, event | category | flops | bytes accessed | tf_op | source)
XLA Modules:
  0.0 254.9 jit_solution(1002400979341382376)
XLA Ops:
  0.0 170.8 %shard_map.28 = (bf16[24,1024,256]{2,1,0:T(8,128)(2,1)}, bf16[2048,8192]{1,0:T(8,128)(2,1)}, bf16[1024,2048]{1,0:T(8,128)(2,1)}, f32[2,1024,8192]{2,1,0:T(8,128)}) custom-call(bf16[5120,1280]{1,0:T(8,128)(2,1)} %l_ref.3, bf16[5,2,512,8192]{3,2,1,0:T(8,128)(2,1)} %bitcast.1.b_ref), custom_call_target="tpu_custom_call" | custom-call | tf_op jit(solution)/shard_map/pallas_call | solution.py:487
  170.8 83.9 %shard_map.29 = bf16[5120,8192]{1,0:T(8,128)(2,1)} custom-call(bf16[5120,1280]{1,0:T(8,128)(2,1)} %l_ref.3, bf16[20,256,8192]{2,1,0:T(8,128)(2,1)} %bitcast.b_ref, bf16[24,1024,256]{2,1,0:T(8,128)(2,1)} %get-tuple-element.8.lg_ref, bf16[2048,8192]{1,0:T(8,128)(2,1)} %get-tuple-element.9.x1_ref, bf16[1024,2048]{1,0:T(8,128)(2,1)} %get-tuple-element.10.x2_ref), custom_call_target="tpu_custom_call" | custom-call | tf_op jit(solution)/shard_map/pallas_call | solution.py:508
